TPU v7x, 32 devices: a whole 2x2x4 slice. The times are simulated.
32 devices in a mesh: dp: 2 (over core), fsdp: 16 (over z, y, x).
Axes of the slice: x: 2, y: 2, z: 4, core: 2. Of those that a mesh axis runs over, the one named last changes fastest.
Arguments:
- tokens: bfloat16 [2, 32, 576, 768], P(None, ('dp', 'fsdp')), may hold values from -6 to 6
- near_bucket: int32 [2, 32, 576, 576], P(None, ('dp', 'fsdp')), may hold values from 0 to 31
- x_bucket: int32 [2, 32, 576, 576], P(None, ('dp', 'fsdp')), may hold values from 0 to 63
- y_bucket: int32 [2, 32, 576, 576], P(None, ('dp', 'fsdp')), may hold values from 0 to 63
- key_mask: int32 [2, 32, 576], P(None, ('dp', 'fsdp')), may hold values 0 or 1
- out_grad: bfloat16 [2, 32, 576, 768], P(None, ('dp', 'fsdp')), may hold values from -6 to 6
- w_query: bfloat16 [768, 768], P(('dp', 'fsdp')), may hold values from -0.21875 to 0.21875
- w_key: bfloat16 [768, 768], P(('dp', 'fsdp')), may hold values from -0.21875 to 0.21875
- w_value: bfloat16 [768, 768], P(('dp', 'fsdp')), may hold values from -0.21875 to 0.21875
- w_out: bfloat16 [768, 768], P(('dp', 'fsdp')), may hold values from -1.75 to 1.75
- w_up: bfloat16 [768, 3072], P(('dp', 'fsdp')), may hold values from -0.21875 to 0.21875
- w_down: bfloat16 [3072, 768], P(('dp', 'fsdp')), may hold values from -0.109375 to 0.109375
- b_query: bfloat16 [768], P(('dp', 'fsdp')), may hold values from -3 to 3
- b_value: bfloat16 [768], P(('dp', 'fsdp')), may hold values from -3 to 3
- b_out: bfloat16 [768], P(('dp', 'fsdp')), may hold values from -3 to 3
- gain_first: bfloat16 [768], P(('dp', 'fsdp')), may hold values from 0.099609375 to 1.8984375
- shift_first: bfloat16 [768], P(('dp', 'fsdp')), may hold values from -3 to 3
- b_up: bfloat16 [3072], P(('dp', 'fsdp')), may hold values from -3 to 3
- b_down: bfloat16 [768], P(('dp', 'fsdp')), may hold values from -3 to 3
- gain_second: bfloat16 [768], P(('dp', 'fsdp')), may hold values from 0.099609375 to 1.8984375
- shift_second: bfloat16 [768], P(('dp', 'fsdp')), may hold values from -3 to 3
- table_near: bfloat16 [32, 12], P('fsdp'), may hold values from -6 to 6
- table_x: bfloat16 [64, 12], P('fsdp'), may hold values from -6 to 6
- table_y: bfloat16 [64, 12], P('fsdp'), may hold values from -6 to 6
Outputs:
- layer_out: bfloat16 [2, 32, 576, 768], P(None, ('dp', 'fsdp'))
- grad_tokens: bfloat16 [2, 32, 576, 768], P(None, ('dp', 'fsdp'))
- grad_w_query: float32 [768, 768], P(('dp', 'fsdp'))
- grad_w_key: float32 [768, 768], P(('dp', 'fsdp'))
- grad_w_value: float32 [768, 768], P(('dp', 'fsdp'))
- grad_w_out: float32 [768, 768], P(('dp', 'fsdp'))
- grad_w_up: float32 [768, 3072], P(('dp', 'fsdp'))
- grad_w_down: float32 [3072, 768], P(('dp', 'fsdp'))
- grad_b_query: float32 [768], P(('dp', 'fsdp'))
- grad_b_value: float32 [768], P(('dp', 'fsdp'))
- grad_b_out: float32 [768], P(('dp', 'fsdp'))
- grad_gain_first: float32 [768], P(('dp', 'fsdp'))
- grad_shift_first: float32 [768], P(('dp', 'fsdp'))
- grad_b_up: float32 [3072], P(('dp', 'fsdp'))
- grad_b_down: float32 [768], P(('dp', 'fsdp'))
- grad_gain_second: float32 [768], P(('dp', 'fsdp'))
- grad_shift_second: float32 [768], P(('dp', 'fsdp'))
- grad_table_near: float32 [32, 12], P('fsdp')
- grad_table_x: float32 [64, 12], P('fsdp')
- grad_table_y: float32 [64, 12], P('fsdp')
All inputs are finite; a program needn't handle non-finite values. No bound on the sum of `key_mask` on one device may be relied on, other than what follows from the above.
Results may differ from a plain program's by a relative error of at most 0.015.
Values may be sent and summed in bfloat16 or wider, within the bound.
A program may use at most 384 MiB of HBM per device.

v0:
```python
import jax
import jax.numpy as jnp
from jax import lax
from jax.sharding import PartitionSpec as P


def layer_norm(inputs, gain_vec, shift_vec):
    average = jnp.mean(inputs, axis=-1, keepdims=True)
    center = inputs - average
    spread_sq = jnp.mean(center * center, axis=-1, keepdims=True)
    return center * lax.rsqrt(spread_sq + 1e-05) * gain_vec + shift_vec


def gelu_exact(inputs):
    return jax.nn.gelu(inputs, approximate=False)


def contract(pattern, left_side, right_side):
    return jnp.einsum(pattern, left_side, right_side, preferred_element_type=jnp.float32)


def onehot_of(buckets, levels):
    level_ids = lax.broadcasted_iota(jnp.int32, (levels, 1, 1, 1), 0)
    return (buckets[None] == level_ids).astype(jnp.bfloat16)


def relative_bias(bucket_sets, tables):
    stride = bucket_sets[0].shape[1] // 3
    portions = []
    for block_index in range(3):
        row_start = block_index * stride
        portion = None
        for bucket_ids, table in zip(bucket_sets, tables):
            rows = bucket_ids[:, row_start : row_start + stride]
            term = contract("bplm,bh->phlm", onehot_of(rows, table.shape[0]), table)
            portion = term if portion is None else portion + term
        portions.append(portion)
    return jnp.concatenate(portions, axis=2)


def table_terms(bucket_sets, d_scores, levels):
    stride = bucket_sets[0].shape[1] // 3
    head_count = d_scores.shape[1]
    sums = [jnp.zeros((level_count, head_count), jnp.float32) for level_count in levels]
    for block_index in range(3):
        row_start = block_index * stride
        block_grads = d_scores[:, :, row_start : row_start + stride]
        for which in range(len(levels)):
            rows = bucket_sets[which][:, row_start : row_start + stride]
            sums[which] = sums[which] + contract(
                "bplm,phlm->bh", onehot_of(rows, levels[which]), block_grads
            )
    return tuple(sums)


def scores_of(query_heads, key_heads, rel_bias, allowed):
    logits = contract("plhe,pmhe->phlm", query_heads, key_heads) * 0.125
    return jnp.where(allowed[:, None], logits + rel_bias, -1e30)


def forward(weights, tables, tokens, bucket_sets, mask_rows):
    (
        w_query,
        w_key,
        w_value,
        w_out,
        w_up,
        w_down,
        b_query,
        b_value,
        b_out,
        gain_first,
        shift_first,
        b_up,
        b_down,
        gain_second,
        shift_second,
    ) = weights
    page_count, length, feature_count = tokens.shape
    head_count = tables[0].shape[1]
    split_shape = (page_count, length, head_count, feature_count // head_count)
    flat_tokens = tokens.reshape(page_count * length, feature_count)
    queries = (jnp.dot(flat_tokens, w_query, preferred_element_type=jnp.float32) + b_query).astype(
        jnp.bfloat16
    )
    key_rows = jnp.dot(flat_tokens, w_key, preferred_element_type=jnp.float32).astype(jnp.bfloat16)
    values = (jnp.dot(flat_tokens, w_value, preferred_element_type=jnp.float32) + b_value).astype(
        jnp.bfloat16
    )
    positions = lax.broadcasted_iota(jnp.int32, (length, length), 0)
    columns = lax.broadcasted_iota(jnp.int32, (length, length), 1)
    allowed = (mask_rows[:, None, :] > 0) | (positions == columns)[None]
    rel_bias = relative_bias(bucket_sets, tables)
    scores = scores_of(
        queries.reshape(split_shape), key_rows.reshape(split_shape), rel_bias, allowed
    )
    row_peak = jnp.max(scores, axis=-1, keepdims=True)
    log_total = row_peak + jnp.log(jnp.sum(jnp.exp(scores - row_peak), axis=-1, keepdims=True))
    probs_low = jnp.exp(scores - log_total).astype(jnp.bfloat16)
    context = contract("phlm,pmhe->plhe", probs_low, values.reshape(split_shape))
    context = context.reshape(page_count * length, feature_count).astype(jnp.bfloat16)
    first_in = flat_tokens + (jnp.dot(context, w_out, preferred_element_type=jnp.float32) + b_out)
    normed_one = layer_norm(
        first_in, gain_first.astype(jnp.float32), shift_first.astype(jnp.float32)
    )
    normed_low = normed_one.astype(jnp.bfloat16)
    hidden_pre = jnp.dot(normed_low, w_up, preferred_element_type=jnp.float32) + b_up
    hidden = gelu_exact(hidden_pre).astype(jnp.bfloat16)
    second_in = normed_one + (jnp.dot(hidden, w_down, preferred_element_type=jnp.float32) + b_down)
    return (
        queries,
        key_rows,
        values,
        allowed,
        rel_bias,
        log_total,
        context,
        first_in,
        normed_low,
        hidden_pre,
        hidden,
        second_in,
    )


def backward(weights, kept_state, tokens, bucket_sets, cotangent, levels):
    (
        w_query,
        w_key,
        w_value,
        w_out,
        w_up,
        w_down,
        b_query,
        b_value,
        b_out,
        gain_first,
        shift_first,
        b_up,
        b_down,
        gain_second,
        shift_second,
    ) = weights
    (
        queries,
        key_rows,
        values,
        allowed,
        rel_bias,
        log_total,
        context,
        first_in,
        normed_low,
        hidden_pre,
        hidden,
        second_in,
    ) = kept_state
    page_count, length, feature_count = tokens.shape
    head_count = log_total.shape[1]
    split_shape = (page_count, length, head_count, feature_count // head_count)
    flat_tokens = tokens.reshape(page_count * length, feature_count)
    layer_value, second_pull = jax.vjp(
        layer_norm, second_in, gain_second.astype(jnp.float32), shift_second.astype(jnp.float32)
    )
    d_second, grad_gain_second, grad_shift_second = second_pull(
        cotangent.reshape(page_count * length, feature_count).astype(jnp.float32)
    )
    d_ffn = d_second.astype(jnp.bfloat16)
    grad_w_down = contract("rf,rd->fd", hidden, d_ffn)
    grad_b_down = jnp.sum(d_ffn.astype(jnp.float32), axis=0)
    d_hidden = contract("rd,fd->rf", d_ffn, w_down)
    gelu_pull = jax.vjp(gelu_exact, hidden_pre)[1]
    d_hidden_pre = gelu_pull(d_hidden)[0].astype(jnp.bfloat16)
    grad_w_up = contract("rd,rf->df", normed_low, d_hidden_pre)
    grad_b_up = jnp.sum(d_hidden_pre.astype(jnp.float32), axis=0)
    d_normed = d_second + contract("rf,df->rd", d_hidden_pre, w_up)
    first_pull = jax.vjp(
        layer_norm, first_in, gain_first.astype(jnp.float32), shift_first.astype(jnp.float32)
    )[1]
    d_first, grad_gain_first, grad_shift_first = first_pull(d_normed)
    d_attn = d_first.astype(jnp.bfloat16)
    grad_w_out = contract("rc,rd->cd", context, d_attn)
    grad_b_out = jnp.sum(d_attn.astype(jnp.float32), axis=0)
    d_context = contract("rd,cd->rc", d_attn, w_out).astype(jnp.bfloat16).reshape(split_shape)
    query_heads = queries.reshape(split_shape)
    key_heads = key_rows.reshape(split_shape)
    value_heads = values.reshape(split_shape)
    scores = scores_of(query_heads, key_heads, rel_bias, allowed)
    attn_probs = jnp.exp(scores - log_total)
    probs_low = attn_probs.astype(jnp.bfloat16)
    d_values = contract("phlm,plhe->pmhe", probs_low, d_context).astype(jnp.bfloat16)
    d_probs = contract("plhe,pmhe->phlm", d_context, value_heads)
    d_scores = (
        attn_probs * (d_probs - jnp.sum(attn_probs * d_probs, axis=-1, keepdims=True))
    ).astype(jnp.bfloat16)
    d_queries = (contract("phlm,pmhe->plhe", d_scores, key_heads) * 0.125).astype(jnp.bfloat16)
    d_keys = (contract("phlm,plhe->pmhe", d_scores, query_heads) * 0.125).astype(jnp.bfloat16)
    table_grads = table_terms(bucket_sets, d_scores, levels)
    d_queries = d_queries.reshape(page_count * length, feature_count)
    d_keys = d_keys.reshape(page_count * length, feature_count)
    d_values = d_values.reshape(page_count * length, feature_count)
    grad_w_query = contract("rd,re->de", flat_tokens, d_queries)
    grad_w_key = contract("rd,re->de", flat_tokens, d_keys)
    grad_w_value = contract("rd,re->de", flat_tokens, d_values)
    grad_b_query = jnp.sum(d_queries.astype(jnp.float32), axis=0)
    grad_b_value = jnp.sum(d_values.astype(jnp.float32), axis=0)
    d_tokens = d_first + contract("re,de->rd", d_queries, w_query)
    d_tokens = d_tokens + contract("re,de->rd", d_keys, w_key)
    d_tokens = d_tokens + contract("re,de->rd", d_values, w_value)
    weight_grads = (
        grad_w_query,
        grad_w_key,
        grad_w_value,
        grad_w_out,
        grad_w_up,
        grad_w_down,
        grad_b_query,
        grad_b_value,
        grad_b_out,
        grad_gain_first,
        grad_shift_first,
        grad_b_up,
        grad_b_down,
        grad_gain_second,
        grad_shift_second,
    )
    return (
        layer_value.astype(jnp.bfloat16).reshape(tokens.shape),
        d_tokens.astype(jnp.bfloat16).reshape(tokens.shape),
        weight_grads,
        table_grads,
    )


def body(
    tokens,
    near_bucket,
    x_bucket,
    y_bucket,
    key_mask,
    out_grad,
    w_query,
    w_key,
    w_value,
    w_out,
    w_up,
    w_down,
    b_query,
    b_value,
    b_out,
    gain_first,
    shift_first,
    b_up,
    b_down,
    gain_second,
    shift_second,
    table_near,
    table_x,
    table_y,
):
    shards = (
        w_query,
        w_key,
        w_value,
        w_out,
        w_up,
        w_down,
        b_query,
        b_value,
        b_out,
        gain_first,
        shift_first,
        b_up,
        b_down,
        gain_second,
        shift_second,
    )
    tables = (
        lax.all_gather(table_near, "fsdp", axis=0, tiled=True),
        lax.all_gather(table_x, "fsdp", axis=0, tiled=True),
        lax.all_gather(table_y, "fsdp", axis=0, tiled=True),
    )
    levels = (tables[0].shape[0], tables[1].shape[0], tables[2].shape[0])
    outputs = []
    input_grads = []
    weight_sums = None
    table_totals = tuple((jnp.zeros(table.shape, jnp.float32) for table in tables))
    for micro_index in range(tokens.shape[0]):
        bucket_sets = (near_bucket[micro_index], x_bucket[micro_index], y_bucket[micro_index])
        weights = (
            lax.all_gather(shards[0], ("dp", "fsdp"), axis=0, tiled=True),
            lax.all_gather(shards[1], ("dp", "fsdp"), axis=0, tiled=True),
            lax.all_gather(shards[2], ("dp", "fsdp"), axis=0, tiled=True),
            lax.all_gather(shards[3], ("dp", "fsdp"), axis=0, tiled=True),
            lax.all_gather(shards[4], ("dp", "fsdp"), axis=0, tiled=True),
            lax.all_gather(shards[5], ("dp", "fsdp"), axis=0, tiled=True),
            lax.all_gather(shards[6], ("dp", "fsdp"), axis=0, tiled=True),
            lax.all_gather(shards[7], ("dp", "fsdp"), axis=0, tiled=True),
            lax.all_gather(shards[8], ("dp", "fsdp"), axis=0, tiled=True),
            lax.all_gather(shards[9], ("dp", "fsdp"), axis=0, tiled=True),
            lax.all_gather(shards[10], ("dp", "fsdp"), axis=0, tiled=True),
            lax.all_gather(shards[11], ("dp", "fsdp"), axis=0, tiled=True),
            lax.all_gather(shards[12], ("dp", "fsdp"), axis=0, tiled=True),
            lax.all_gather(shards[13], ("dp", "fsdp"), axis=0, tiled=True),
            lax.all_gather(shards[14], ("dp", "fsdp"), axis=0, tiled=True),
        )
        kept_state = forward(
            weights, tables, tokens[micro_index], bucket_sets, key_mask[micro_index]
        )
        fenced = lax.optimization_barrier((shards, kept_state))[0]
        weights_back = (
            lax.all_gather(fenced[0], ("dp", "fsdp"), axis=0, tiled=True),
            lax.all_gather(fenced[1], ("dp", "fsdp"), axis=0, tiled=True),
            lax.all_gather(fenced[2], ("dp", "fsdp"), axis=0, tiled=True),
            lax.all_gather(fenced[3], ("dp", "fsdp"), axis=0, tiled=True),
            lax.all_gather(fenced[4], ("dp", "fsdp"), axis=0, tiled=True),
            lax.all_gather(fenced[5], ("dp", "fsdp"), axis=0, tiled=True),
            lax.all_gather(fenced[6], ("dp", "fsdp"), axis=0, tiled=True),
            lax.all_gather(fenced[7], ("dp", "fsdp"), axis=0, tiled=True),
            lax.all_gather(fenced[8], ("dp", "fsdp"), axis=0, tiled=True),
            lax.all_gather(fenced[9], ("dp", "fsdp"), axis=0, tiled=True),
            lax.all_gather(fenced[10], ("dp", "fsdp"), axis=0, tiled=True),
            lax.all_gather(fenced[11], ("dp", "fsdp"), axis=0, tiled=True),
            lax.all_gather(fenced[12], ("dp", "fsdp"), axis=0, tiled=True),
            lax.all_gather(fenced[13], ("dp", "fsdp"), axis=0, tiled=True),
            lax.all_gather(fenced[14], ("dp", "fsdp"), axis=0, tiled=True),
        )
        layer_part, grad_part, weight_grads, table_parts = backward(
            weights_back,
            kept_state,
            tokens[micro_index],
            bucket_sets,
            out_grad[micro_index],
            levels,
        )
        outputs.append(layer_part)
        input_grads.append(grad_part)
        table_totals = tuple((summed + latest for summed, latest in zip(table_totals, table_parts)))
        shares = (
            lax.psum_scatter(weight_grads[0], ("dp", "fsdp"), scatter_dimension=0, tiled=True),
            lax.psum_scatter(weight_grads[1], ("dp", "fsdp"), scatter_dimension=0, tiled=True),
            lax.psum_scatter(weight_grads[2], ("dp", "fsdp"), scatter_dimension=0, tiled=True),
            lax.psum_scatter(weight_grads[3], ("dp", "fsdp"), scatter_dimension=0, tiled=True),
            lax.psum_scatter(weight_grads[4], ("dp", "fsdp"), scatter_dimension=0, tiled=True),
            lax.psum_scatter(weight_grads[5], ("dp", "fsdp"), scatter_dimension=0, tiled=True),
            lax.psum_scatter(weight_grads[6], ("dp", "fsdp"), scatter_dimension=0, tiled=True),
            lax.psum_scatter(weight_grads[7], ("dp", "fsdp"), scatter_dimension=0, tiled=True),
            lax.psum_scatter(weight_grads[8], ("dp", "fsdp"), scatter_dimension=0, tiled=True),
            lax.psum_scatter(weight_grads[9], ("dp", "fsdp"), scatter_dimension=0, tiled=True),
            lax.psum_scatter(weight_grads[10], ("dp", "fsdp"), scatter_dimension=0, tiled=True),
            lax.psum_scatter(weight_grads[11], ("dp", "fsdp"), scatter_dimension=0, tiled=True),
            lax.psum_scatter(weight_grads[12], ("dp", "fsdp"), scatter_dimension=0, tiled=True),
            lax.psum_scatter(weight_grads[13], ("dp", "fsdp"), scatter_dimension=0, tiled=True),
            lax.psum_scatter(weight_grads[14], ("dp", "fsdp"), scatter_dimension=0, tiled=True),
        )
        if weight_sums is None:
            weight_sums = shares
        else:
            weight_sums = tuple((summed + latest for summed, latest in zip(weight_sums, shares)))
    table_sums = lax.psum((table_totals[0], table_totals[1], table_totals[2]), ("dp", "fsdp"))
    fsdp_rank = lax.axis_index("fsdp")
    near_count = table_near.shape[0]
    plane_count = table_x.shape[0]
    near_share = lax.dynamic_slice_in_dim(table_sums[0], fsdp_rank * near_count, near_count, 0)
    x_share = lax.dynamic_slice_in_dim(table_sums[1], fsdp_rank * plane_count, plane_count, 0)
    y_share = lax.dynamic_slice_in_dim(table_sums[2], fsdp_rank * plane_count, plane_count, 0)
    return (
        (jnp.stack(outputs), jnp.stack(input_grads))
        + tuple(weight_sums)
        + (near_share, x_share, y_share)
    )


def solution(mesh):
    return jax.shard_map(
        body,
        mesh=mesh,
        in_specs=(
            P(None, ("dp", "fsdp"), None, None),
            P(None, ("dp", "fsdp"), None, None),
            P(None, ("dp", "fsdp"), None, None),
            P(None, ("dp", "fsdp"), None, None),
            P(None, ("dp", "fsdp"), None),
            P(None, ("dp", "fsdp"), None, None),
            P(("dp", "fsdp"), None),
            P(("dp", "fsdp"), None),
            P(("dp", "fsdp"), None),
            P(("dp", "fsdp"), None),
            P(("dp", "fsdp"), None),
            P(("dp", "fsdp"), None),
            P(("dp", "fsdp")),
            P(("dp", "fsdp")),
            P(("dp", "fsdp")),
            P(("dp", "fsdp")),
            P(("dp", "fsdp")),
            P(("dp", "fsdp")),
            P(("dp", "fsdp")),
            P(("dp", "fsdp")),
            P(("dp", "fsdp")),
            P("fsdp", None),
            P("fsdp", None),
            P("fsdp", None),
        ),
        out_specs=(
            P(None, ("dp", "fsdp"), None, None),
            P(None, ("dp", "fsdp"), None, None),
            P(("dp", "fsdp"), None),
            P(("dp", "fsdp"), None),
            P(("dp", "fsdp"), None),
            P(("dp", "fsdp"), None),
            P(("dp", "fsdp"), None),
            P(("dp", "fsdp"), None),
            P(("dp", "fsdp")),
            P(("dp", "fsdp")),
            P(("dp", "fsdp")),
            P(("dp", "fsdp")),
            P(("dp", "fsdp")),
            P(("dp", "fsdp")),
            P(("dp", "fsdp")),
            P(("dp", "fsdp")),
            P(("dp", "fsdp")),
            P("fsdp", None),
            P("fsdp", None),
            P("fsdp", None),
        ),
        check_vma=False,
    )
```

profile of v0, /device:TPU:0, one launch (start us, length us, event | category | flops | bytes accessed | tf_op | source)
XLA Modules:
  0.0 1935.7 jit_solution(5881545911593813029)
XLA Ops:
  17.1 42.4 %all-reduce.24 = (bf16[768]{0:T(1024)(128)(2,1)S(1)}, bf16[768]{0:T(1024)(128)(2,1)S(1)}, bf16[768]{0:T(1024)(128)(2,1)S(1)}, bf16[768]{0:T(1024)(128)(2,1)S(1)}...) all-reduce(bf16[768]{0:T(1024)(128)(2,1)S(1)} %dynamic-update-slice, ...), channel_id=1, replica_groups=mesh['dp'=2,'fsdp'=16] {'dp','fsdp'}, use_global_device_ids=true, to_apply=%add | all-reduce | flops 7680 | bytes 30720
  60.7 39.6 %all-gather.2 = bf16[16,4,12]{2,1,0:T(4,128)(2,1)S(1)} all-gather(bf16[1,4,12]{2,1,0:T(4,128)(2,1)} %bitcast.452), channel_id=1, replica_groups=mesh['dp'=2,'fsdp'=16] {'fsdp'}, dimensions={0}, use_global_device_ids=true | all-gather | bytes 1632 | tf_op jit(solution)/shard_map/all_gather | solution.py:281
  102.5 35.5 %all-gather.1 = bf16[16,4,12]{2,1,0:T(4,128)(2,1)S(1)} all-gather(bf16[1,4,12]{2,1,0:T(4,128)(2,1)S(1)} %bitcast.453), channel_id=1, replica_groups=mesh['dp'=2,'fsdp'=16] {'fsdp'}, dimensions={0}, use_global_device_ids=true | all-gather | bytes 1632 | tf_op jit(solution)/shard_map/all_gather | solution.py:280
  138.3 37.5 %all-gather = bf16[16,2,12]{2,1,0:T(2,128)(2,1)S(1)} all-gather(bf16[1,2,12]{2,1,0:T(2,128)(2,1)S(1)} %bitcast.454), channel_id=1, replica_groups=mesh['dp'=2,'fsdp'=16] {'fsdp'}, dimensions={0}, use_global_device_ids=true | all-gather | bytes 816 | tf_op jit(solution)/shard_map/all_gather | solution.py:279
  306.9 15.4 fusion.91
  322.3 15.5 fusion.92
  337.8 15.3 fusion.93
  353.1 15.3 fusion.88
  368.5 15.4 fusion.89
  383.8 15.2 fusion.90
  414.2 15.9 fusion.288
  464.7 12.9 fusion.290
  497.5 21.6 %multiply_convert_fusion.2 = (bf16[576,3072]{1,0:T(8,128)(2,1)}, f32[576,3072]{1,0:T(8,128)}, f32[576,3072]{1,0:T(8,128)}) fusion(f32[3072]{0:T(1024)} %convert_element_type.315, bf16[576,768]{1,0:T(8,128)(2,1)} %get-tuple-element.217, bf16[768,3072]{1,0:T(8,128)(2,1)} %all-gather.30.cloned.1.call-done), kind=kOutput, calls=%fused_computation.112 | convolution fusion | flops 2834694144 | bytes 23310336 | tf_op jit(solution)/shard_map/dot_general | solution.py:107
  528.9 21.1 %multiply_convert_fusion.3 = (bf16[576,3072]{1,0:T(8,128)(2,1)S(1)}, f32[576,3072]{1,0:T(8,128)}, f32[576,3072]{1,0:T(8,128)}) fusion(f32[3072]{0:T(1024)} %convert_element_type.315, bf16[576,768]{1,0:T(8,128)(2,1)} %get-tuple-element.216, bf16[768,3072]{1,0:T(8,128)(2,1)} %all-gather.30.cloned.1.call-done), kind=kOutput, calls=%fused_computation.125 | convolution fusion | flops 2834694144 | bytes 23310336 | tf_op jit(solution)/shard_map/dot_general | solution.py:107
  567.1 38.1 %all-reduce.23 = (bf16[768]{0:T(1024)(128)(2,1)}, bf16[768]{0:T(1024)(128)(2,1)}, bf16[768]{0:T(1024)(128)(2,1)}, bf16[768]{0:T(1024)(128)(2,1)}, bf16[768]{0:T(1024)(128)(2,1)}, /*index=5*/bf16[768]{0:T(1024)(128)(2,1)}) all-reduce(bf16[768]{0:T(1024)(128)(2,1)S(1)} %dynamic-update-slice.10, ...), channel_id=1, replica_groups=mesh['dp'=2,'fsdp'=16] {'dp','fsdp'}, use_global_device_ids=true, to_apply=%add.10 | all-reduce | flops 4608 | bytes 18432
  631.8 12.7 convert_reduce_fusion
  664.5 43.4 %all-gather.50.cloned.1.call-done = bf16[768,768]{1,0:T(8,128)(2,1)} async-done(((bf16[24,768]{1,0:T(8,128)(2,1)}), bf16[768,768]{1,0:T(8,128)(2,1)}) %all-gather.50.cloned.1.call-update) | async-done | bytes 1179664 | tf_op jit(solution)/shard_map/all_gather | solution.py:315
  713.5 13.3 multiply_reduce_fusion
  726.8 46.4 %all-gather.34.cloned.1.call-done = bf16[3072,768]{1,0:T(8,128)(2,1)} async-done(((bf16[96,768]{1,0:T(8,128)(2,1)}), bf16[3072,768]{1,0:T(8,128)(2,1)}) %all-gather.34.cloned.1.call-update) | async-done | bytes 4718608 | tf_op jit(solution)/shard_map/all_gather | solution.py:317
  773.1 12.2 convert_reduce_fusion.1
  785.3 52.6 %all-gather.36.cloned.1.call-done = bf16[768,3072]{1,0:T(8,128)(2,1)} async-done(((bf16[24,3072]{1,0:T(8,128)(2,1)}), bf16[768,3072]{1,0:T(8,128)(2,1)}) %all-gather.36.cloned.1.call-update) | async-done | bytes 4718608 | tf_op jit(solution)/shard_map/all_gather | solution.py:316
  848.0 44.9 %all-gather.38.cloned.1.call-done = bf16[768,768]{1,0:T(8,128)(2,1)} async-done(((bf16[24,768]{1,0:T(8,128)(2,1)}), bf16[768,768]{1,0:T(8,128)(2,1)}) %all-gather.38.cloned.1.call-update) | async-done | bytes 1179664 | tf_op jit(solution)/shard_map/all_gather | solution.py:315
  895.7 15.6 multiply_reduce_fusion.1
  911.3 16.4 multiply_convert_fusion.1
  939.6 11.2 multiply_convert_fusion
  1173.9 41.7 %all-reduce.22 = (f32[768]{0:T(1024)S(1)}, f32[768]{0:T(1024)S(1)}, f32[768]{0:T(1024)S(1)}, f32[768]{0:T(1024)S(1)}, f32[768]{0:T(1024)S(1)}, /*index=5*/f32[30...) all-reduce(f32[768]{0:T(1024)S(1)} %reshape.678, ...), channel_id=23, replica_groups=mesh['dp'=2,'fsdp'=16] {'dp','fsdp'}, use_global_device_ids=true, to_apply=%region_35.36.clone | all-reduce | flops 11136 | bytes 89088
  1247.6 83.9 %reduce-scatter.19.cloned.1.call-done = f32[24,768]{1,0:T(8,128)} async-done(((f32[768,768]{1,0:T(8,128)}), f32[24,768]{1,0:T(8,128)}) %reduce-scatter.19.cloned.1.call-update) | async-done | bytes 73744
  1331.5 104.5 %reduce-scatter.21.cloned.1.call-done = f32[24,768]{1,0:T(8,128)} async-done(((f32[768,768]{1,0:T(8,128)}), f32[24,768]{1,0:T(8,128)}) %reduce-scatter.21.cloned.1.call-update) | async-done | bytes 73744
  1436.0 104.6 %reduce-scatter.23.cloned.1.call-done = f32[24,768]{1,0:T(8,128)} async-done(((f32[768,768]{1,0:T(8,128)}), f32[24,768]{1,0:T(8,128)}) %reduce-scatter.23.cloned.1.call-update) | async-done | bytes 73744
  1540.5 104.4 %reduce-scatter.13.cloned.1.call-done = f32[24,768]{1,0:T(8,128)} async-done(((f32[768,768]{1,0:T(8,128)}), f32[24,768]{1,0:T(8,128)}) %reduce-scatter.13.cloned.1.call-update) | async-done | bytes 73744 | tf_op jit(solution)/shard_map/reduce_scatter | solution.py:343
  1645.0 141.8 %reduce-scatter.17.cloned.1.call-done = f32[96,768]{1,0:T(8,128)} async-done(((f32[3072,768]{1,0:T(8,128)}), f32[96,768]{1,0:T(8,128)}) %reduce-scatter.17.cloned.1.call-update) | async-done | bytes 294928 | tf_op jit(solution)/shard_map/reduce_scatter | solution.py:345
  1786.8 141.8 %reduce-scatter.15.cloned.1.call-done = f32[24,3072]{1,0:T(8,128)} async-done(((f32[768,3072]{1,0:T(8,128)}), f32[24,3072]{1,0:T(8,128)}) %reduce-scatter.15.cloned.1.call-update) | async-done | bytes 294928 | tf_op jit(solution)/shard_map/reduce_scatter | solution.py:344
  (583 shorter events, 570.9 us)
Async XLA Ops:
  7.2 95.3 %copy-start.148 = (bf16[4,12]{1,0:T(4,128)(2,1)S(1)}, bf16[4,12]{1,0:T(4,128)(2,1)}, u32[]{:S(2)}) copy-start(bf16[4,12]{1,0:T(4,128)(2,1)} %param.46) | copy-start | bytes 292
  7.2 130.9 %copy-start.72 = (s32[2,1,576,576]{3,2,1,0:T(8,128)S(1)}, s32[2,1,576,576]{3,2,1,0:T(8,128)}, u32[]{:S(2)}) copy-start(s32[2,1,576,576]{3,2,1,0:T(8,128)} %param.26) | copy-start | bytes 7962628
  7.2 391.9 %all-gather.22.cloned.1.call-start = ((), (), s32[]{:S(2)}) async-start(), calls=%async_computation.6 | async-start | bytes 1216512 | tf_op jit(solution)/shard_map/all_gather | solution.py:293
  7.9 395.7 %all-gather.24.cloned.1.call-start = ((), (), s32[]{:S(2)}) async-start(), calls=%async_computation.7 | async-start | bytes 1216512 | tf_op jit(solution)/shard_map/all_gather | solution.py:291
  8.7 400.3 %all-gather.26.cloned.1.call-start = ((), (), s32[]{:S(2)}) async-start(), calls=%async_computation.8 | async-start | bytes 1216512 | tf_op jit(solution)/shard_map/all_gather | solution.py:292
  9.4 437.4 %all-gather.28.cloned.1.call-start = ((), (), s32[]{:S(2)}) async-start(), calls=%async_computation.9 | async-start | bytes 1216512 | tf_op jit(solution)/shard_map/all_gather | solution.py:294
  10.0 487.5 %all-gather.30.cloned.1.call-start = ((), (), s32[]{:S(2)}) async-start(), calls=%async_computation.10 | async-start | bytes 4866048 | tf_op jit(solution)/shard_map/all_gather | solution.py:295
  10.6 508.5 %all-gather.32.cloned.1.call-start = ((), (), s32[]{:S(2)}) async-start(), calls=%async_computation.11 | async-start | bytes 4866048 | tf_op jit(solution)/shard_map/all_gather | solution.py:296
  11.2 620.6 %all-gather.46.cloned.1.call-start = ((), (), s32[]{:S(2)}) async-start(), calls=%async_computation.18 | async-start | bytes 4866048 | tf_op jit(solution)/shard_map/all_gather | solution.py:317
  176.2 86.8 %copy-start.50 = (s32[192,576]{1,0:T(8,128)}, s32[192,576]{1,0:T(8,128)S(1)}, u32[]{:S(2)}) copy-start(s32[192,576]{1,0:T(8,128)S(1)} %get-tuple-element.215) | copy-start | bytes 1327108
  176.3 108.4 %copy-start.58 = (s32[192,576]{1,0:T(8,128)}, s32[192,576]{1,0:T(8,128)S(1)}, u32[]{:S(2)}) copy-start(s32[192,576]{1,0:T(8,128)S(1)} %get-tuple-element.213) | copy-start | bytes 1327108
  191.9 79.1 %copy-start.62 = (s32[192,576]{1,0:T(8,128)}, s32[192,576]{1,0:T(8,128)S(1)}, u32[]{:S(2)}) copy-start(s32[192,576]{1,0:T(8,128)S(1)} %get-tuple-element.212) | copy-start | bytes 1327108
  191.9 100.3 %copy-start.68 = (s32[192,576]{1,0:T(8,128)}, s32[192,576]{1,0:T(8,128)S(1)}, u32[]{:S(2)}) copy-start(s32[192,576]{1,0:T(8,128)S(1)} %get-tuple-element.210) | copy-start | bytes 1327108
  207.5 92.6 %copy-start.86 = (s32[192,576]{1,0:T(8,128)}, s32[192,576]{1,0:T(8,128)S(1)}, u32[]{:S(2)}) copy-start(s32[192,576]{1,0:T(8,128)S(1)} %get-tuple-element.207) | copy-start | bytes 1327108
  527.3 125.4 %all-gather.48.cloned.1.call-start = ((), (), s32[]{:S(2)}) async-start(), calls=%async_computation.19 | async-start | bytes 4866048 | tf_op jit(solution)/shard_map/all_gather | solution.py:316
  528.1 179.8 %all-gather.50.cloned.1.call-start = ((), (), s32[]{:S(2)}) async-start(), calls=%async_computation.20 | async-start | bytes 1216512 | tf_op jit(solution)/shard_map/all_gather | solution.py:315
  528.8 244.3 %all-gather.34.cloned.1.call-start = ((), (), s32[]{:S(2)}) async-start(), calls=%async_computation.12 | async-start | bytes 4866048 | tf_op jit(solution)/shard_map/all_gather | solution.py:317
  554.9 283.0 %all-gather.36.cloned.1.call-start = ((), (), s32[]{:S(2)}) async-start(), calls=%async_computation.13 | async-start | bytes 4866048 | tf_op jit(solution)/shard_map/all_gather | solution.py:316
  555.6 337.3 %all-gather.38.cloned.1.call-start = ((), (), s32[]{:S(2)}) async-start(), calls=%async_computation.14 | async-start | bytes 1216512 | tf_op jit(solution)/shard_map/all_gather | solution.py:315
  556.2 666.4 %all-gather.54.cloned.1.call-start = ((), (), s32[]{:S(2)}) async-start(), calls=%async_computation.22 | async-start | bytes 1216512 | tf_op jit(solution)/shard_map/all_gather | solution.py:313
  556.9 669.2 %all-gather.52.cloned.1.call-start = ((), (), s32[]{:S(2)}) async-start(), calls=%async_computation.21 | async-start | bytes 1216512 | tf_op jit(solution)/shard_map/all_gather | solution.py:312
  557.5 672.2 %all-gather.42.cloned.1.call-start = ((), (), s32[]{:S(2)}) async-start(), calls=%async_computation.16 | async-start | bytes 1216512 | tf_op jit(solution)/shard_map/all_gather | solution.py:313
  558.1 675.3 %all-gather.40.cloned.1.call-start = ((), (), s32[]{:S(2)}) async-start(), calls=%async_computation.15 | async-start | bytes 1216512 | tf_op jit(solution)/shard_map/all_gather | solution.py:312
  558.7 678.6 %all-gather.56.cloned.1.call-start = ((), (), s32[]{:S(2)}) async-start(), calls=%async_computation.23 | async-start | bytes 1216512 | tf_op jit(solution)/shard_map/all_gather | solution.py:314
  619.1 623.1 %all-gather.44.cloned.1.call-start = ((), (), s32[]{:S(2)}) async-start(), calls=%async_computation.17 | async-start | bytes 1216512 | tf_op jit(solution)/shard_map/all_gather | solution.py:314
  631.6 699.9 %reduce-scatter.19.cloned.1.call-start = ((), (), s32[]{:S(2)}) async-start(), calls=%async_computation.27 | async-start | bytes 2433024
  961.3 474.7 %reduce-scatter.21.cloned.1.call-start = ((), (), s32[]{:S(2)}) async-start(), calls=%async_computation.28 | async-start | bytes 2433024
  978.4 562.1 %reduce-scatter.23.cloned.1.call-start = ((), (), s32[]{:S(2)}) async-start(), calls=%async_computation.29 | async-start | bytes 2433024
  1001.9 643.1 %reduce-scatter.13.cloned.1.call-start = ((), (), s32[]{:S(2)}) async-start(), calls=%async_computation.24 | async-start | bytes 2433024 | tf_op jit(solution)/shard_map/reduce_scatter | solution.py:343
  1006.9 779.9 %reduce-scatter.17.cloned.1.call-start = ((), (), s32[]{:S(2)}) async-start(), calls=%async_computation.26 | async-start | bytes 9732096 | tf_op jit(solution)/shard_map/reduce_scatter | solution.py:345
  1020.3 908.3 %reduce-scatter.15.cloned.1.call-start = ((), (), s32[]{:S(2)}) async-start(), calls=%async_computation.25 | async-start | bytes 9732096 | tf_op jit(solution)/shard_map/reduce_scatter | solution.py:344
  1041.2 116.2 %copy-start.74 = (bf16[12,192,576]{2,1,0:T(8,128)(2,1)}, bf16[12,192,576]{2,1,0:T(8,128)(2,1)S(1)}, u32[]{:S(2)}) copy-start(bf16[12,192,576]{2,1,0:T(8,128)(2,1)S(1)} %get-tuple-element.181) | copy-start | bytes 7962628
  (154 other events, 2328.3 us)
Sparse Core Ops, SparseCore 0:
  10.9 56.9 all-gather.21
  70.8 52.8 all-gather.23
  126.6 52.7 all-gather.25
  182.1 52.9 all-gather.27
  237.9 62.4 all-gather.29
  303.1 61.8 all-gather.31
  527.5 60.0 all-gather.45
  590.4 62.2 all-gather.47
  655.6 52.2 all-gather.49
  710.7 62.4 all-gather.33
  776.0 61.8 all-gather.35
  840.6 52.2 all-gather.37
  895.8 52.8 all-gather.53
  951.5 52.8 all-gather.51
  1007.1 52.8 all-gather.41
  1062.8 52.8 all-gather.39
  1118.4 52.9 all-gather.55
  1174.1 52.9 all-gather.43
  1232.9 98.4 reduce-scatter.18
  1337.2 98.7 reduce-scatter.20
  1441.8 98.6 reduce-scatter.22
  1546.4 98.5 reduce-scatter.12
  1651.5 135.3 reduce-scatter.16
  1793.2 135.4 reduce-scatter.14
where the time goes:
time: 1940 us
  waiting for transfers between devices  885 us (46%)
  matrix products  554 us (29%)
  blocking collectives  235 us (12%)
  other arithmetic  177 us (9%)
  local copies, waits for them, and re-layouts  66.1 us (3%)
    dot_general x72, matrix products, contract(): jnp.einsum(pattern, left_side, right_side, preferred_element_type=jnp.flo...  476 us
    unnamed x27, waiting for transfers between devices  302 us
    reduce_scatter x1, waiting for transfers between devices, body(): lax.psum_scatter(weight_grads[5], ('dp', 'fsdp'), scatter_dimension=0, ti...  142 us
    reduce_scatter x1, waiting for transfers between devices, body(): lax.psum_scatter(weight_grads[4], ('dp', 'fsdp'), scatter_dimension=0, ti...  142 us
    unnamed x3, blocking collectives  122 us
    reduce_scatter x1, waiting for transfers between devices, body(): lax.psum_scatter(weight_grads[3], ('dp', 'fsdp'), scatter_dimension=0, ti...  104 us
    add x6, other arithmetic, relative_bias(): portion = term if portion is None else portion + term  92.2 us
    all_gather x2, waiting for transfers between devices, body(): lax.all_gather(fenced[3], ('dp', 'fsdp'), axis=0, tiled=True)  88.3 us
  transfers between devices with their start and end apart: 24, of which 11 were waited for; matrix products, arithmetic and copies ran while one was open for 40% of the time, Pallas kernels for 0%

commit v1 on v0

v1 whole, which is shorter than its diff:
```python
import functools
import jax
import jax.numpy as jnp
from jax import lax
from jax.experimental import pallas as pl
from jax.experimental.pallas import tpu as pltpu
from jax.sharding import PartitionSpec as P

BF, F32 = jnp.bfloat16, jnp.float32
NN = (((1,), (0,)), ((), ()))
NT = (((1,), (1,)), ((), ()))
TN = (((0,), (0,)), ((), ()))


def mm(left, right, dims=NN):
    return lax.dot_general(left, right, dims, preferred_element_type=F32)


def bias_kernel(near_ref, x_ref, y_ref, mask_ref, tab_ref, out_ref, *, heads, length):
    rows = near_ref.shape[1]
    base = pl.program_id(1) * rows

    def group(r, carry):
        start = pl.multiple_of(r * 8, 8)
        for lane in range(0, length, 128):
            width = min(128, length - lane)
            ids = []
            line = base + start + lax.broadcasted_iota(jnp.int32, (8, width), 0)
            column = lane + lax.broadcasted_iota(jnp.int32, (8, width), 1)
            allowed = (mask_ref[0, :, lane : lane + width] > 0) | (line == column)
            for which, ref in enumerate((near_ref, x_ref, y_ref)):
                part = ref[0, pl.ds(start, 8), lane : lane + width]
                if which == 0:
                    part = jnp.where(allowed, part, 127)
                if width < 128:
                    part = jnp.concatenate([part, jnp.zeros((8, 128 - width), jnp.int32)], axis=1)
                ids.append(part)
            sums = [None] * heads
            for which in range(3):
                for h in range(heads):
                    row = jnp.broadcast_to(tab_ref[which, h : h + 1, :], (8, 128))
                    got = jnp.take_along_axis(row, ids[which], axis=1)
                    sums[h] = got if which == 0 else sums[h] + got
            for h in range(heads):
                out_ref[0, h, pl.ds(start, 8), lane : lane + width] = sums[h][:, :width]
        return carry

    lax.fori_loop(0, rows // 8, group, 0)


def relative_bias(near, xb, yb, mask, tabs, rows=96):
    pages, length, _ = near.shape
    heads = tabs.shape[1]
    idx = pl.BlockSpec((1, rows, length), lambda p, r: (p, r, 0))
    return pl.pallas_call(
        functools.partial(bias_kernel, heads=heads, length=length),
        grid=(pages, length // rows),
        in_specs=[idx, idx, idx, pl.BlockSpec((1, 1, length), lambda p, r: (p, 0, 0)),
                  pl.BlockSpec((3, heads, 128), lambda p, r: (0, 0, 0))],
        out_specs=pl.BlockSpec((1, heads, rows, length), lambda p, r: (p, 0, r, 0)),
        out_shape=jax.ShapeDtypeStruct((pages, heads, length, length), F32),
        name="bias",
        cost_estimate=pl.CostEstimate(flops=30_000_000, bytes_accessed=60_000_000, transcendentals=0),
    )(near, xb, yb, mask, tabs)


def fwd_kernel(q_ref, k_ref, v_ref, bias_ref, e_ref, ctx_ref, inv_ref, *, rows):
    length = q_ref.shape[0]
    low_half = lax.broadcasted_iota(jnp.int32, (1, 128), 1) < 64
    keys = k_ref[...]
    values = v_ref[...]
    zero, one = jnp.zeros((), BF), jnp.ones((), BF)
    v_ext = (jnp.where(low_half, values, one), jnp.where(low_half, one, values))

    def chunk(c, carry):
        at = pl.ds(pl.multiple_of(c * rows, rows), rows)
        q = q_ref[at, :]
        q_sel = (jnp.where(low_half, q, zero), jnp.where(low_half, zero, q))
        outs = []
        for j in range(2):
            s = mm(q_sel[j], keys, NT) + bias_ref[0, j, at, :]
            e = jnp.exp(s - jnp.max(s, axis=1, keepdims=True)).astype(BF)
            e_ref[0, j, at, :] = e
            outs.append(mm(e, v_ext[j]))
        total = pltpu.roll(jnp.where(low_half, outs[1], outs[0]), 64, 1)
        inv = 1.0 / total
        inv_ref[at, :] = inv
        ctx_ref[at, :] = jnp.where(low_half, outs[0], outs[1]) * inv
        return carry

    lax.fori_loop(0, length // rows, chunk, 0)


def attention_fwd(q, k, v, bias, rows=96):
    pages, heads, length, _ = bias.shape
    feat = q.shape[1]
    tok = pl.BlockSpec((length, 128), lambda p, h: (p, h))
    mat = pl.BlockSpec((1, 2, length, length), lambda p, h: (p, h, 0, 0))
    return pl.pallas_call(
        functools.partial(fwd_kernel, rows=rows),
        grid=(pages, heads // 2),
        in_specs=[tok, tok, tok, mat],
        out_specs=[mat, tok, tok],
        out_shape=[jax.ShapeDtypeStruct(bias.shape, BF), jax.ShapeDtypeStruct(q.shape, F32), jax.ShapeDtypeStruct(q.shape, F32)],
        name="attn_fwd",
        cost_estimate=pl.CostEstimate(flops=4 * pages * length * length * feat, bytes_accessed=60_000_000, transcendentals=pages * heads * length * length),
    )(q, k, v, bias)


def bwd_kernel(e_ref, q_ref, k_ref, v_ref, do_ref, ctx_ref, dq_ref, dk_ref, dv_ref, ds_ref, *, rows, small_t):
    length = q_ref.shape[0]
    low_half = lax.broadcasted_iota(jnp.int32, (1, 128), 1) < 64
    keys = k_ref[...]
    values = v_ref[...]
    zero = jnp.zeros((), BF)

    def chunk(c, carry):
        at = pl.ds(pl.multiple_of(c * rows, rows), rows)
        do = do_ref[at, :]
        prod = do.astype(F32) * ctx_ref[at, :]
        outs = []
        for j in range(2):
            mine = low_half if j == 0 else jnp.logical_not(low_half)
            delta = jnp.sum(jnp.where(mine, prod, 0.0), axis=1, keepdims=True)
            dp = mm(jnp.where(mine, do, zero), values, NT)
            ds = (e_ref[0, j, at, :].astype(F32) * (dp - delta)).astype(BF)
            ds_ref[0, j, at, :] = ds
            outs.append(mm(ds, keys))
        dq_ref[at, :] = (jnp.where(low_half, outs[0], outs[1]) * 0.125).astype(BF)
        return carry

    lax.fori_loop(0, length // rows, chunk, 0)
    for src, other, dst in ((ds_ref, q_ref, dk_ref), (e_ref, do_ref, dv_ref)):
        if small_t:
            other_t = other[...].T
            top = mm(other_t[:64], src[0, 0])
            bottom = mm(other_t[64:], src[0, 1])
            dst[...] = jnp.concatenate([top, bottom], axis=0).astype(BF).T
        else:
            dst[...] = jnp.where(low_half, mm(src[0, 0], other[...], TN), mm(src[0, 1], other[...], TN)).astype(BF)


def attention_bwd(e, q, k, v, do, ctx, rows=96, small_t=True):
    pages, heads, length, _ = e.shape
    feat = q.shape[1]
    tok = pl.BlockSpec((length, 128), lambda p, h: (p, h))
    mat = pl.BlockSpec((1, 2, length, length), lambda p, h: (p, h, 0, 0))
    return pl.pallas_call(
        functools.partial(bwd_kernel, rows=rows, small_t=small_t),
        grid=(pages, heads // 2),
        in_specs=[mat, tok, tok, tok, tok, tok],
        out_specs=[tok, tok, tok, mat],
        out_shape=[jax.ShapeDtypeStruct(q.shape, BF)] * 3 + [jax.ShapeDtypeStruct(e.shape, BF)],
        name="attn_bwd",
        cost_estimate=pl.CostEstimate(flops=8 * pages * length * length * feat, bytes_accessed=50_000_000, transcendentals=0),
    )(e, q, k, v, do, ctx)


def hist_kernel(near_ref, x_ref, y_ref, ds_ref, out_ref, stage, *, heads, levels):
    group, length = near_ref.shape[1], near_ref.shape[2]
    tiles = -(-length // 128)
    spare = tiles * 128 - length

    @pl.when((pl.program_id(0) == 0) & (pl.program_id(1) == 0))
    def _():
        out_ref[...] = jnp.zeros_like(out_ref)
        for t in range(tiles):
            for r in range(group):
                stage[t, pl.ds(r * 16 + 8, 8), :] = jnp.zeros((8, 128), F32)

    for h in range(heads):
        part = ds_ref[0, h].astype(F32)
        if spare:
            part = jnp.concatenate([part, jnp.zeros((group, spare), F32)], axis=1)
        for t in range(tiles):
            for r in range(0, group, 8):
                stage[t, pl.ds(r * 16 + h, 8, 16), :] = part[r : r + 8, t * 128 : (t + 1) * 128]

    total = jnp.zeros(out_ref.shape, F32)
    for r in range(group):
        marks = []
        for ref, level in zip((near_ref, x_ref, y_ref), levels):
            row = jnp.broadcast_to(ref[0, r : r + 1, :], (level, length))
            marks.append((row == lax.broadcasted_iota(jnp.int32, (level, length), 0)).astype(F32).astype(BF))
        grads = jnp.concatenate([stage[t, pl.ds(r * 16, 16), :].astype(BF) for t in range(tiles)], axis=1)
        total = total + mm(grads[:, :length], jnp.concatenate(marks, axis=0), NT)
    out_ref[...] += total


def table_hist(near, xb, yb, ds, levels, group=16):
    pages, heads, length, _ = ds.shape
    idx = pl.BlockSpec((1, group, length), lambda p, r: (p, r, 0))
    return pl.pallas_call(
        functools.partial(hist_kernel, heads=heads, levels=levels),
        grid=(pages, length // group),
        in_specs=[idx, idx, idx, pl.BlockSpec((1, heads, group, length), lambda p, r: (p, 0, r, 0))],
        out_specs=pl.BlockSpec((16, sum(levels)), lambda p, r: (0, 0)),
        out_shape=jax.ShapeDtypeStruct((16, sum(levels)), F32),
        scratch_shapes=[pltpu.VMEM((-(-length // 128), group * 16, 128), F32)],
        name="hist",
        cost_estimate=pl.CostEstimate(flops=3_000_000_000, bytes_accessed=30_000_000, transcendentals=0),
    )(near, xb, yb, ds)


def gelu_pair(u):
    bell = jnp.exp(-0.5 * u * u)
    phi = 0.5 * (1.0 + lax.erf(u * 0.7071067811865476))
    return u * phi, phi + u * bell * 0.3989422804014327


def norm_parts(rows):
    center = rows - jnp.mean(rows, axis=-1, keepdims=True)
    scale = lax.rsqrt(jnp.mean(center * center, axis=-1, keepdims=True) + 1e-05)
    return center * scale, scale


def norm_back(cot, xhat, scale, gain):
    gc = cot * gain
    return scale * (gc - jnp.mean(gc, axis=-1, keepdims=True) - xhat * jnp.mean(gc * xhat, axis=-1, keepdims=True))


def small_pack(vectors, rows):
    flat = jnp.concatenate([v.reshape(-1) for v in vectors])
    return jnp.pad(flat, (0, rows * 128 - flat.shape[0])).reshape(rows, 128)


AXES = ("dp", "fsdp")


def body(tokens, near, xb, yb, key_mask, out_grad, w_query, w_key, w_value, w_out, w_up, w_down,
         b_query, b_value, b_out, gain_first, shift_first, b_up, b_down, gain_second, shift_second,
         table_near, table_x, table_y):
    micro, pages, length, feat = tokens.shape
    heads = table_near.shape[1]
    own = w_query.shape[0]
    ff = w_up.shape[1]
    count = feat // own
    fsdp = lax.axis_size("fsdp")
    merged = micro * pages
    rows = merged * length
    vectors = (b_query, b_value, b_out, gain_first, shift_first, b_down, gain_second, shift_second, b_up)
    tables = (table_near, table_x, table_y)
    small = small_pack(vectors + tables, own)
    first = lax.all_gather(jnp.concatenate([w_query, w_key, w_value, small], axis=1), AXES, axis=0, tiled=True)
    second = lax.all_gather(jnp.concatenate([w_out, w_up], axis=1), AXES, axis=0, tiled=True)
    w_down_all = lax.all_gather(w_down, AXES, axis=0, tiled=True)
    w_qkv = first[:, : 3 * feat]
    smalls = first[:, 3 * feat :].reshape(count, own * 128)
    at = 0
    full = []
    for v in vectors:
        full.append(smalls[:, at : at + v.shape[0]].reshape(1, -1).astype(F32))
        at += v.shape[0]
    bq, bv, bo, g1, s1, bd, g2, s2, bu = full
    tabs = []
    for which, t in enumerate(tables):
        n = t.shape[0] * fsdp
        full_t = smalls[:fsdp, at : at + t.size].reshape(n, heads).T.astype(F32)
        full_t = jnp.pad(full_t, ((0, 0), (0, 128 - n)))
        if which == 0:
            full_t = full_t.at[:, 127].set(-1e30)
        tabs.append(full_t)
        at += t.size
    levels = tuple(t.shape[0] * fsdp for t in tables)

    near, xb, yb = (a.reshape(merged, length, length) for a in (near, xb, yb))
    mask = key_mask.reshape(merged, 1, length)
    tok = tokens.reshape(rows, feat)
    cot = out_grad.reshape(rows, feat).astype(F32)
    rel_bias = relative_bias(near, xb, yb, mask, jnp.stack(tabs))
    qkv = mm(tok, w_qkv)
    q = (qkv[:, :feat] + bq).astype(BF)
    qs = q * jnp.asarray(0.125, BF)
    k = qkv[:, feat : 2 * feat].astype(BF)
    v = (qkv[:, 2 * feat :] + bv).astype(BF)
    e, ctx, inv = attention_fwd(qs, k, v, rel_bias)
    ctx_low = ctx.astype(BF)
    w_o, w_u = second[:, :feat], second[:, feat:]
    x1, r1 = norm_parts(tok.astype(F32) + (mm(ctx_low, w_o) + bo))
    normed = x1 * g1 + s1
    normed_low = normed.astype(BF)
    hidden, slope = gelu_pair(mm(normed_low, w_u) + bu)
    hidden = hidden.astype(BF)
    slope = slope.astype(BF)
    x2, r2 = norm_parts(normed + (mm(hidden, w_down_all) + bd))
    layer_out = (x2 * g2 + s2).astype(BF)
    d_second = norm_back(cot, x2, r2, g2)
    d_ffn = d_second.astype(BF)
    gw_down = mm(hidden, d_ffn, TN)
    d_pre = (mm(d_ffn, w_down_all, NT) * slope.astype(F32)).astype(BF)
    gw_up = mm(normed_low, d_pre, TN)
    d_normed = d_second + mm(d_pre, w_u, NT)
    d_first = norm_back(d_normed, x1, r1, g1)
    d_attn = d_first.astype(BF)
    gw_out = mm(ctx_low, d_attn, TN)
    d_ctx = (mm(d_attn, w_o, NT) * inv).astype(BF)
    down_share = lax.psum_scatter(gw_down.astype(BF), AXES, scatter_dimension=0, tiled=True)
    up_share = lax.psum_scatter(jnp.concatenate([gw_out.astype(BF), gw_up.astype(BF)], axis=1), AXES, scatter_dimension=0, tiled=True)
    dq, dk, dv, ds = attention_bwd(e, qs, k, v, d_ctx, ctx)
    dqkv = jnp.concatenate([dq, dk, dv], axis=1)
    gw_qkv = mm(tok, dqkv, TN)
    col = lambda a: jnp.sum(a.astype(F32), axis=0)
    parts = (col(dq), col(dv), col(d_attn), col(d_normed * x1), col(d_normed), col(d_ffn), col(cot * x2), col(cot), col(d_pre))
    vec_parts = jnp.concatenate([p.reshape(count, -1) for p in parts], axis=1)
    vec_parts = jnp.pad(vec_parts, ((0, 0), (0, own * 128 - vec_parts.shape[1]))).reshape(feat, 128)
    qkv_share = lax.psum_scatter(jnp.concatenate([gw_qkv, jnp.pad(vec_parts, ((0, 0), (0, 128)))], axis=1).astype(BF), AXES, scatter_dimension=0, tiled=True).astype(F32)
    d_tok = (d_first + mm(dqkv, w_qkv, NT)).astype(BF)
    hist = table_hist(near, xb, yb, ds, levels)[:heads].T
    hist = lax.psum(hist, AXES)
    rank = lax.axis_index("fsdp")
    table_shares = []
    at = 0
    for t, n in zip(tables, levels):
        table_shares.append(lax.dynamic_slice_in_dim(hist, at + rank * t.shape[0], t.shape[0], 0))
        at += n
    vec_share = qkv_share[:, 3 * feat : 3 * feat + 128].reshape(-1)
    vec_out = []
    at = 0
    for v_ in vectors:
        vec_out.append(vec_share[at : at + v_.shape[0]])
        at += v_.shape[0]
    v_bq, v_bv, v_bo, v_g1, v_s1, v_bd, v_g2, v_s2, v_bu = vec_out
    up_share = up_share.astype(F32)
    return (layer_out.reshape(tokens.shape), d_tok.reshape(tokens.shape),
            qkv_share[:, :feat], qkv_share[:, feat : 2 * feat], qkv_share[:, 2 * feat : 3 * feat],
            up_share[:, :feat], up_share[:, feat:], down_share.astype(F32),
            v_bq, v_bv, v_bo, v_g1, v_s1, v_bu, v_bd, v_g2, v_s2, *table_shares)


def solution(mesh):
    pages = P(None, AXES, None, None)
    mat, vec, tab = P(AXES, None), P(AXES), P("fsdp", None)
    return jax.shard_map(
        body,
        mesh=mesh,
        in_specs=(pages,) * 4 + (P(None, AXES, None), pages) + (mat,) * 6 + (vec,) * 9 + (tab,) * 3,
        out_specs=(pages,) * 2 + (mat,) * 6 + (vec,) * 9 + (tab,) * 3,
        check_vma=False,
    )
```

time: 1940 us -> 718 us (0.37)
  waiting for transfers between devices: 885 us -> 210 us
  matrix products: 554 us -> 108 us
  Pallas kernels: 0 us -> 252 us
  blocking collectives: 235 us -> 39.3 us
  other arithmetic: 177 us -> 32.4 us
    dot_general x84 -> x12, matrix products: 554 us -> 108 us  [mm(): return lax.dot_general(left, right, dims, preferred_element_type=F32)]
    unnamed x27 -> x6, waiting for transfers between devices: 302 us -> 0.76 us
    pallas_call x0 -> x4, Pallas kernels: none -> 252 us  [the longest x1 91 us: table_hist(): pl.pallas_call(functools.partial(hist_kernel, heads=heads, levels=levels)...]
    reduce_scatter x3, waiting for transfers between devices: 388 us -> 150 us  [the longest x1 116 us: body(): lax.psum_scatter(jnp.concatenate([gw_out.astype(BF), gw_up.astype(BF)], a...]
    all_gather x18 -> x3, waiting for transfers between devices: 196 us -> 59.2 us  [the longest x1 59.2 us: body(): lax.all_gather(jnp.concatenate([w_query, w_key, w_value, small], axis=1),...]
    unnamed x3 -> x0, blocking collectives: 122 us -> none
    all_gather x3 -> x0, blocking collectives: 113 us -> none  [the longest x1 39.6 us: body(): lax.all_gather(table_y, 'fsdp', axis=0, tiled=True)]
    add x17 -> x0, other arithmetic: 96.1 us -> none  [the longest x6 92.2 us: relative_bias(): portion = term if portion is None else portion + term]
  transfers between devices with their start and end apart: 24 -> 6, of which waited for: 11 -> 3; matrix products, arithmetic and copies ran while one was open for 40% -> 12% of each run, Pallas kernels for 0% -> 29%
where the time goes in v1:
time: 718 us; the launch traced here: 708 us
  Pallas kernels  252 us (35%)
  waiting for transfers between devices  210 us (29%)
  matrix products  108 us (15%)
  local copies, waits for them, and re-layouts  51.3 us (7%)
  blocking collectives  39.3 us (5%)
  other arithmetic  32.4 us (5%)
  between operations  14.7 us (2%)
    reduce_scatter x1, waiting for transfers between devices, body(): lax.psum_scatter(jnp.concatenate([gw_out.astype(BF), gw_up.astype(BF)], a...  116 us
    dot_general x12, matrix products, mm(): return lax.dot_general(left, right, dims, preferred_element_type=F32)  108 us
    pallas_call x1, Pallas kernels, table_hist(): pl.pallas_call(functools.partial(hist_kernel, heads=heads, levels=levels)...  91 us
    pallas_call x1, Pallas kernels, attention_fwd(): pl.pallas_call(functools.partial(fwd_kernel, rows=rows), grid=(pages, hea...  63.3 us
    all_gather x1, waiting for transfers between devices, body(): lax.all_gather(jnp.concatenate([w_query, w_key, w_value, small], axis=1),...  59.2 us
    pallas_call x1, Pallas kernels, attention_bwd(): pl.pallas_call(functools.partial(bwd_kernel, rows=rows, small_t=small_t),...  49.6 us
    pallas_call x1, Pallas kernels, relative_bias(): pl.pallas_call(functools.partial(bias_kernel, heads=heads, length=length)...  48 us
    psum x1, blocking collectives, body(): hist = lax.psum(hist, AXES)  39.3 us
  transfers between devices with their start and end apart: 6, of which 3 were waited for; matrix products, arithmetic and copies ran while one was open for 12% of the time, Pallas kernels for 29%

profile of v1, /device:TPU:0, one launch (start us, length us, event | category | flops | bytes accessed | tf_op | source)
XLA Modules:
  0.0 707.9 jit_solution(5975659639367198641)
XLA Ops:
  9.6 6.1 concatenate.25
  19.7 1.8 reduce.9
  21.6 59.2 %all-gather.4.cloned.1.call-done = bf16[768,2432]{1,0:T(8,128)(2,1)} async-done(((bf16[24,2432]{1,0:T(8,128)(2,1)}), bf16[768,2432]{1,0:T(8,128)(2,1)}) %all-gather.4.cloned.1.call-update) | async-done | bytes 3735568 | tf_op jit(solution)/shard_map/all_gather | solution.py:244
  84.7 48.0 %bias.1.bias_ref = f32[2,12,576,576]{3,2,1,0:T(8,128)} custom-call(s32[2,576,576]{2,1,0:T(8,128)} %bitcast.59, s32[2,576,576]{2,1,0:T(8,128)} %bitcast.61, s32[2,576,576]{2,1,0:T(8,128)} %bitcast.63, s32[2,1,576]{2,1,0:T(1,128)} %mask_ref.1, f32[3,12,128]{2,1,0:T(8,128)} %pad_maximum_fusion.3.tab_ref), custom_call_target="tpu_custom_call" | custom-call | flops 30000000 | bytes 60000000 | tf_op jit(solution)/shard_map/bias/pallas_call | solution.py:55
  132.7 6.9 convolution_bitcast_fusion
  141.2 2.3 fusion.43
  143.6 63.3 %attn_fwd.1 = (bf16[2,12,576,576]{3,2,1,0:T(8,128)(2,1)}, f32[1152,768]{1,0:T(8,128)}, f32[1152,768]{1,0:T(8,128)}) custom-call(bf16[1152,768]{1,0:T(8,128)(2,1)} %get-tuple-element.117.q_ref, bf16[1152,768]{1,0:T(8,128)(2,1)} %get-tuple-element.116.k_ref, bf16[1152,768]{1,0:T(8,128)(2,1)} %fusion.17.v_ref, f32[2,12,576,576]{3,2,1,0:T(8,128)} %bias.1.bias_ref), custom_call_target="tpu_custom_call" | custom-call | flops 2038431744 | bytes 60000000 | tf_op jit(solution)/shard_map/attn_fwd/pallas_call | solution.py:99
  206.9 4.9 fusion.49
  213.6 11.3 %multiply_convert_fusion = (bf16[1152,3072]{1,0:T(8,128)(2,1)}, f32[1152,3072]{1,0:T(8,128)}) fusion(f32[3072]{0:T(1024)S(1)} %reshape.326, bf16[768,3840]{1,0:T(8,128)(2,1)S(1)} %bitcast.67, f32[1152,768]{1,0:T(8,128)S(1)} %get-tuple-element.147, f32[768]{0:T(1024)S(1)} %reshape.325, f32[768]{0:T(1024)S(1)} %reshape.324, f32[1152]{0:T(1024)S(1)} %add_rsqrt_fusion.1, ...), kind=kOutput, calls=%fused_computation.7 | convolution fusion | flops 5461475328 | bytes 29528064 | tf_op jit(solution)/shard_map/dot_general | solution.py:16
  224.9 11.9 %fusion.50 = (f32[1152]{0:T(1024)S(1)}, f32[1152,768]{1,0:T(8,128)S(1)}) fusion(f32[768]{0:T(1024)S(1)} %reshape.327, bf16[1152,3072]{1,0:T(8,128)(2,1)} %get-tuple-element.148, bf16[3072,768]{1,0:T(8,128)(2,1)} %all-gather.8.cloned.1.call-done, f32[768]{0:T(1024)S(1)} %reshape.325, f32[768]{0:T(1024)S(1)} %reshape.324, f32[1152]{0:T(1024)S(1)} %add_rsqrt_fusion.1, ...), kind=kOutput, calls=%fused_computation.111 | convolution fusion | flops 5442010112 | bytes 18897408 | tf_op jit(solution)/shard_map/dot_general | solution.py:16
  237.3 3.6 fusion.25
  241.0 1.9 convert_reduce_fusion.1
  242.9 16.8 %fusion.51 = (bf16[3072]{0:T(1024)(128)(2,1)}, bf16[1152,3072]{1,0:T(8,128)(2,1)}) fusion(f32[1152,3072]{1,0:T(8,128)} %get-tuple-element.149, bf16[3072,768]{1,0:T(8,128)(2,1)S(1)} %bitcast.74, f32[1152,768]{1,0:T(8,128)S(1)} %get-tuple-element.113), kind=kOutput, calls=%fused_computation.112 | convolution fusion | flops 5482705920 | bytes 29497344 | tf_op jit(solution)/shard_map/dot_general | solution.py:16
  259.7 10.6 %multiply_reduce_fusion = (bf16[768]{0:T(1024)(128)(2,1)}, f32[1152]{0:T(1024)S(1)}, f32[1152]{0:T(1024)S(1)}, bf16[768]{0:T(1024)(128)(2,1)}, f32[1152,768]{1,0:T(8,128)S(1)}) fusion(f32[1152,768]{1,0:T(8,128)S(1)} %copy-done.2, f32[1152]{0:T(1024)S(1)} %add_rsqrt_fusion.1, f32[1152]{0:T(1024)S(1)} %broadcast_multiply_fusion.4, f32[768]{0:T(1024)S(1)} %reshape.324, ...), kind=kOutput, calls=%fused_computation.45 | convolution fusion | flops 5444661248 | bytes 22446080 | tf_op jit(solution)/shard_map/dot_general | solution.py:16
  270.3 2.9 convert_reduce_fusion
  273.2 2.9 fusion.27.do_ref
  276.1 49.6 %attn_bwd.1 = (bf16[1152,768]{1,0:T(8,128)(2,1)}, bf16[1152,768]{1,0:T(8,128)(2,1)}, bf16[1152,768]{1,0:T(8,128)(2,1)}, bf16[2,12,576,576]{3,2,1,0:T(8,128)(2,1)}) custom-call(bf16[2,12,576,576]{3,2,1,0:T(8,128)(2,1)} %get-tuple-element.40.e_ref, bf16[1152,768]{1,0:T(8,128)(2,1)} %get-tuple-element.117.q_ref, bf16[1152,768]{1,0:T(8,128)(2,1)} %get-tuple-element.116.k_ref, ...), custom_call_target="tpu_custom_call" | custom-call | flops 4076863488 | bytes 50000000 | tf_op jit(solution)/shard_map/attn_bwd/pallas_call | solution.py:148
  325.7 2.7 fusion.45
  329.9 6.5 fusion.7
  352.1 1.7 copy.73
  353.8 3.7 fusion.11
  357.4 6.3 copy.82
  363.8 11.1 %convolution_convert_fusion = bf16[3072,768]{1,0:T(8,128)(2,1)} fusion(bf16[1152,3072]{1,0:T(8,128)(2,1)} %get-tuple-element.148, f32[1152,768]{1,0:T(8,128)} %copy-done.4), kind=kOutput, calls=%fused_computation.15 | convolution fusion | flops 5439062016 | bytes 15335424 | tf_op jit(solution)/shard_map/dot_general | solution.py:16
  375.0 4.8 convolution_convert_fusion.3
  379.8 2.4 copy.75
  382.2 10.7 %convolution_convert_fusion.1 = bf16[768,3072]{1,0:T(8,128)(2,1)S(1)} fusion(bf16[1152,3072]{1,0:T(8,128)(2,1)} %get-tuple-element.154, f32[1152,768]{1,0:T(8,128)} %copy-done.1, f32[768]{0:T(1024)} %copy-done.12, f32[768]{0:T(1024)} %copy-done.11, f32[1152]{0:T(1024)S(1)} %copy-done.10, f32[1152]{0:T(1024)S(1)} %broadcast_multiply_fusion.4), kind=kOutput, calls=%fused_computation.16 | convolution fusion | flops 5442600960 | bytes 15350784 | tf_op jit(solution)/shard_map/dot_general | solution.py:16
  393.0 2.9 pad_maximum_fusion
  395.9 91.0 %hist.1 = f32[16,160]{1,0:T(8,128)} custom-call(s32[2,576,576]{2,1,0:T(8,128)} %bitcast.60, s32[2,576,576]{2,1,0:T(8,128)} %bitcast.62, s32[2,576,576]{2,1,0:T(8,128)} %bitcast.64, bf16[2,12,576,576]{3,2,1,0:T(8,128)(2,1)} %get-tuple-element.45.ds_ref), custom_call_target="tpu_custom_call" | custom-call | flops 3000000000 | bytes 30000000 | tf_op jit(solution)/shard_map/hist/pallas_call | solution.py:193
  488.3 39.3 %psum.7 = f32[160,12]{0,1:T(8,128)S(1)} all-reduce(f32[160,12]{0,1:T(8,128)} %slice_bitcast_fusion), channel_id=1, replica_groups=mesh['dp'=2,'fsdp'=16] {'dp','fsdp'}, use_global_device_ids=true, to_apply=%region_20.21 | all-reduce | flops 1920 | bytes 15360 | tf_op jit(solution)/shard_map/psum | solution.py:309
  532.9 9.3 %fusion.26 = bf16[1152,768]{1,0:T(8,128)(2,1)} fusion(f32[1152,768]{1,0:T(8,128)S(1)} %get-tuple-element.115, bf16[1152,2304]{1,0:T(8,128)(2,1)} %copy-done.8, bf16[768,2432]{1,0:T(8,128)(2,1)} %all-gather.4.cloned.1.call-done), kind=kOutput, calls=%fused_computation.52 | convolution fusion | flops 4078632960 | bytes 14155776 | tf_op jit(solution)/shard_map/dot_general | solution.py:16
  545.9 34.2 %reduce-scatter.8.cloned.1.call-done = bf16[96,768]{1,0:T(8,128)(2,1)} async-done(((bf16[3072,768]{1,0:T(8,128)(2,1)}), bf16[96,768]{1,0:T(8,128)(2,1)}) %reduce-scatter.8.cloned.1.call-update) | async-done | bytes 147472 | tf_op jit(solution)/shard_map/reduce_scatter | solution.py:297
  581.7 116.0 %reduce-scatter.6.cloned.1.call-done = bf16[24,3840]{1,0:T(8,128)(2,1)} async-done(((bf16[768,3840]{1,0:T(8,128)(2,1)}), bf16[24,3840]{1,0:T(8,128)(2,1)}) %reduce-scatter.6.cloned.1.call-update) | async-done | bytes 184336 | tf_op jit(solution)/shard_map/reduce_scatter | solution.py:298
  (131 shorter events, 46.5 us)
Async XLA Ops:
  7.2 76.3 %copy-start = (bf16[2,1,576,768]{3,2,1,0:T(8,128)(2,1)S(1)}, bf16[2,1,576,768]{3,2,1,0:T(8,128)(2,1)}, u32[]{:S(2)}) copy-start(bf16[2,1,576,768]{3,2,1,0:T(8,128)(2,1)} %param.31) | copy-start | bytes 5308420
  7.2 73.6 %all-gather.4.cloned.1.call-start = ((), (), s32[]{:S(2)}) async-start(), calls=%async_computation.3 | async-start | bytes 3852288 | tf_op jit(solution)/shard_map/all_gather | solution.py:244
  17.2 189.7 %all-gather.6.cloned.1.call-start = ((), (), s32[]{:S(2)}) async-start(), calls=%async_computation.4 | async-start | bytes 6082560 | tf_op jit(solution)/shard_map/all_gather | solution.py:245
  18.9 206.0 %all-gather.8.cloned.1.call-start = ((), (), s32[]{:S(2)}) async-start(), calls=%async_computation.5 | async-start | bytes 4866048 | tf_op jit(solution)/shard_map/all_gather | solution.py:246
  19.6 522.6 %reduce-scatter.10.cloned.1.call-start = ((), (), s32[]{:S(2)}) async-start(), calls=%async_computation.8 | async-start | bytes 4055040 | tf_op jit(solution)/shard_map/reduce_scatter | solution.py:306
  82.9 176.7 %copy-start.11 = (f32[768]{0:T(1024)}, f32[768]{0:T(1024)S(1)}, u32[]{:S(2)}) copy-start(f32[768]{0:T(1024)S(1)} %reshape.324) | copy-start | bytes 9220
  83.0 141.8 %copy-start.12 = (f32[768]{0:T(1024)}, f32[768]{0:T(1024)S(1)}, u32[]{:S(2)}) copy-start(f32[768]{0:T(1024)S(1)} %reshape.325) | copy-start | bytes 9220
  206.9 6.7 slice-start
  206.9 6.7 slice-start.1
  211.8 1.8 copy-start.1
  213.6 46.1 %copy-start.9 = (f32[1152]{0:T(1024)}, f32[1152]{0:T(1024)S(1)}, u32[]{:S(2)}) copy-start(f32[1152]{0:T(1024)S(1)} %add_rsqrt_fusion.1) | copy-start | bytes 13828
  236.8 6.1 slice-start.4
  237.3 5.5 slice-start.5
  240.9 18.7 %slice-start.2 = ((s8[5898240]{0:T(1024)(128)(4,1)}), s8[4194304]{0:T(1024)(128)(4,1)S(1)}, s32[]{:S(2)}) async-start(s8[5898240]{0:T(1024)(128)(4,1)} %bitcast.68), calls=%async_computation.11 | async-start | bytes 8388608
  242.8 16.8 %copy-start.4 = (f32[1152,768]{1,0:T(8,128)}, f32[1152,768]{1,0:T(8,128)S(1)}, u32[]{:S(2)}) copy-start(f32[1152,768]{1,0:T(8,128)S(1)} %get-tuple-element.113) | copy-start | bytes 10616836
  242.8 16.8 %copy-start.2 = (f32[1152,768]{1,0:T(8,128)S(1)}, f32[1152,768]{1,0:T(8,128)}, u32[]{:S(2)}) copy-start(f32[1152,768]{1,0:T(8,128)} %copy-done.1) | copy-start | bytes 10616836
  242.8 16.8 %slice-start.3 = ((s8[5898240]{0:T(1024)(128)(4,1)}), s8[1703936]{0:T(1024)(128)(4,1)S(1)}, s32[]{:S(2)}) async-start(s8[5898240]{0:T(1024)(128)(4,1)} %bitcast.68), calls=%async_computation.12 | async-start | bytes 3407872
  270.3 2.9 copy-start.5
  325.7 2.7 copy-start.7
  325.7 2.8 copy-start.6
  328.4 1.5 copy-start.13
  329.6 6.8 copy-start.8
  363.8 216.3 %reduce-scatter.8.cloned.1.call-start = ((), (), s32[]{:S(2)}) async-start(), calls=%async_computation.7 | async-start | bytes 4866048 | tf_op jit(solution)/shard_map/reduce_scatter | solution.py:297
  374.9 7.3 %copy-start.10 = (f32[1152]{0:T(1024)S(1)}, f32[1152]{0:T(1024)}, u32[]{:S(2)}) copy-start(f32[1152]{0:T(1024)} %copy-done.9) | copy-start | bytes 13828
  374.9 322.8 %reduce-scatter.6.cloned.1.call-start = ((), (), s32[]{:S(2)}) async-start(), calls=%async_computation.6 | async-start | bytes 6082560 | tf_op jit(solution)/shard_map/reduce_scatter | solution.py:298
  382.2 10.7 %copy-start.3 = (bf16[768,768]{1,0:T(8,128)(2,1)S(1)}, bf16[768,768]{1,0:T(8,128)(2,1)}, u32[]{:S(2)}) copy-start(bf16[768,768]{1,0:T(8,128)(2,1)} %copy.75) | copy-start | bytes 3538948
Sparse Core Ops, SparseCore 0:
  17.3 63.3 all-gather.3
  84.2 66.3 all-gather.5
  153.5 62.7 all-gather.7
  363.9 103.6 reduce-scatter.9
  473.0 107.0 reduce-scatter.7
  585.6 112.1 reduce-scatter.5
